TPU v7x, 128 devices: a whole 4x4x4 slice. The times are simulated.
128 devices in a mesh: rep: 2 (over core), dp: 64 (over x, y, z).
Axes of the slice: x: 4, y: 4, z: 4, core: 2. Of those that a mesh axis runs over, the one named last changes fastest.
Arguments:
- a: bfloat16 [128, 2, 4096, 1024], P(('rep', 'dp')), parts along dimension 0
- g: bfloat16 [128, 2, 4096, 4096], P(('rep', 'dp')), parts along dimension 0
Outputs:
- output: bfloat16 [4, 1024, 4096], P('rep'), parts along dimension 0
There are 2 independent parts. A program takes and returns all parts, laid end to end along the dimension named above; each array names one.
All inputs are finite; a program needn't handle non-finite values.
Results may differ from a plain program's by a relative error of at most 0.012.
Values are sent between devices in bfloat16 or wider.
A program may use at most 1.5 GiB of HBM per device.

v0:
```python
import jax
import jax.numpy as jnp


def solution(mesh):
    groups = mesh.shape["rep"]

    def step(a, g):
        a, g = (t.reshape(groups, -1, *t.shape[1:]) for t in (a, g))
        sums = jnp.einsum("rsntd,rsntf->rndf", a, g, preferred_element_type=jnp.float32)
        return sums.astype(jnp.bfloat16).reshape(-1, *sums.shape[2:])

    return step
```

profile of v0, /device:TPU:0, one launch (start us, length us, event | category | flops | bytes accessed | tf_op | source)
XLA Modules:
  0.0 818.8 jit_solution(18021308445924433073)
XLA Ops:
  0.0 79.2 %fusion.3 = f32[1,2,1024,4096]{3,2,1,0:T(8,128)} fusion(bf16[1,2,4096,4096]{3,2,1,0:T(8,128)(2,1)} %param.1, bf16[1,2,4096,1024]{3,2,1,0:T(8,128)(2,1)} %param), kind=kOutput, calls=%fused_computation.4 | convolution fusion | flops 68719476736 | bytes 117440512 | tf_op jit(solution)/rsntd,rsntf->rndf/dot_general | solution.py:10
  79.2 739.6 %all-reduce.2 = bf16[1,2,1024,4096]{3,2,1,0:T(8,128)(2,1)} all-reduce(f32[1,2,1024,4096]{3,2,1,0:T(8,128)} %fusion.3), channel_id=1, replica_groups=[2,64]<=[128], use_global_device_ids=true, to_apply=%add.clone | all-reduce | flops 8388608 | bytes 50331648 | tf_op jit(solution)/rsntd,rsntf->rndf/dot_general | solution.py:10
where the time goes:
time: 819 us
  blocking collectives  740 us (90%)
  matrix products  79.2 us (10%)
    dot_general x1, blocking collectives, step(): jnp.einsum('rsntd,rsntf->rndf', a, g, preferred_element_type=jnp.float32)  740 us
    dot_general x1, matrix products, step(): jnp.einsum('rsntd,rsntf->rndf', a, g, preferred_element_type=jnp.float32)  79.2 us

commit v1 on v0

v1 whole, which is shorter than its diff:
```python
import functools

import jax
import jax.numpy as jnp
from jax import lax
from jax.experimental import pallas as pl
from jax.experimental.pallas import tpu as pltpu
from jax.sharding import PartitionSpec as P

F32, BF16 = jnp.float32, jnp.bfloat16

WAVE = 1024
NB = 256
SUBS = WAVE // NB
WIDTHS = (384, 384, 256)
STARTS = (0, 384, 768)
SLOTS = 5
GBUF = 3
KB = 512
A_L, A_R, FIN, B_L, B_R, FIN2, RS3, AG3, F2_L, F2_R, REST2, F1_L, F1_R, REST1 = range(14)


def kernel(
    waves, per, a_hbm, g_hbm, out_hbm,
    at, abuf, gbuf, T, R1, R2, R3, O,
    a_sem, g_sem, o_sem, rs_send, ag_send, recv,
):
    rep, me = lax.axis_index("rep"), lax.axis_index("dp")
    x, y, z = me // 16, (me // 4) % 4, me % 4
    tokens = a_hbm.shape[2]

    def place(k):
        p = jnp.where(k == 0, x, jnp.where(k == 1, y, z))
        s = jnp.where(k == 0, 16, jnp.where(k == 1, 4, 1))
        return p, s

    def peer(k, d):
        p, s = place(k)
        return me + ((p + d) % 4 - p) * s

    barrier = pltpu.get_barrier_semaphore()
    for k in range(3):
        for d in (1, 2, 3):
            pl.semaphore_signal(barrier, inc=1, device_id={"dp": peer(k, d)})

    def a_copy(n, i):
        return pltpu.make_async_copy(
            a_hbm.at[0, n, pl.ds(pl.multiple_of(i * KB, KB), KB), :], abuf.at[i % 2], a_sem.at[i % 2]
        )

    def g_copy(j):
        w, s = j // SUBS, j % SUBS
        n = w // per
        col = pl.multiple_of((w % per) * WAVE + s * NB, NB)
        return pltpu.make_async_copy(g_hbm.at[0, n, :, pl.ds(col, NB)], gbuf.at[j % GBUF], g_sem.at[j % GBUF])

    def o_copy(w):
        n = w // per
        col = pl.multiple_of((w % per) * WAVE, WAVE)
        return pltpu.make_async_copy(O.at[w], out_hbm.at[n, :, pl.ds(col, WAVE)], o_sem.at[w])

    def turn(n):
        pieces = tokens // KB

        def piece(i, _):
            a_copy(n, i).wait()
            at[:, pl.ds(pl.multiple_of(i * KB, KB), KB)] = abuf[i % 2].T

            @pl.when(i + 2 < pieces)
            def _():
                a_copy(n, i + 2).start()

            return 0

        lax.fori_loop(0, pieces, piece, 0)

    def send(src, dst, k, d, ssem, rsem):
        pltpu.make_async_remote_copy(
            src_ref=src, dst_ref=dst, send_sem=ssem, recv_sem=rsem, device_id={"dp": peer(k, d)},
        ).start()

    def wait(ref, sem):
        pltpu.make_async_copy(ref, ref, sem).wait()

    def rows(start, size):
        return pl.ds(pl.multiple_of(start, 16), size)

    def add(dst, drow, srcs, n, cols, out=None):
        out = dst if out is None else out
        step = min(n, 64)

        def body(i, _):
            o = i * step
            total = dst[rows(drow + o, step), cols].astype(F32)
            for ref, row in srcs:
                total = total + ref[rows(row + o, step), cols].astype(F32)
            out[rows(drow + o, step), cols] = total.astype(BF16)
            return 0

        if n == step:
            body(0, 0)
        else:
            lax.fori_loop(0, n // step, body, 0)

    def colours(w):
        for c in range(3):
            k0 = (c + w + rep) % 3
            k1, k2 = (k0 + 1) % 3, (k0 + 2) % 3
            yield c, (k0, k1, k2), pl.ds(STARTS[c], WIDTHS[c])

    def rs_first(w, c, k, base, q, t, r, cols, fin):
        p, _ = place(k)
        h = q // 2
        opp, nxt, prv = ((p + i) % 4 for i in (2, 1, 3))
        s = rs_send.at[w]
        al, ar = fin - 2, fin - 1
        send(t.at[rows(base + opp * q, h), cols], r.at[pl.ds(0, h), cols], k, 1, s, recv.at[w, c, al])
        send(t.at[rows(base + opp * q + h, h), cols], r.at[pl.ds(h, h), cols], k, 3, s, recv.at[w, c, ar])
        send(t.at[rows(base + nxt * q + h, h), cols], r.at[pl.ds(3 * h, h), cols], k, 1, s, recv.at[w, c, fin])
        send(t.at[rows(base + prv * q, h), cols], r.at[pl.ds(4 * h, h), cols], k, 3, s, recv.at[w, c, fin])

    def rs_middle(w, c, k, base, q, t, r, cols, fin):
        p, _ = place(k)
        h = q // 2
        nxt, prv = (p + 1) % 4, (p + 3) % 4
        s = rs_send.at[w]
        wait(r.at[pl.ds(0, h), cols], recv.at[w, c, fin - 2])
        add(t, base + nxt * q, [(r, 0)], h, cols)
        wait(r.at[pl.ds(h, h), cols], recv.at[w, c, fin - 1])
        add(t, base + prv * q + h, [(r, h)], h, cols)
        send(t.at[rows(base + nxt * q, h), cols], r.at[pl.ds(2 * h, h), cols], k, 1, s, recv.at[w, c, fin])
        send(t.at[rows(base + prv * q + h, h), cols], r.at[pl.ds(5 * h, h), cols], k, 3, s, recv.at[w, c, fin])

    def rs_last(w, c, k, base, q, t, r, cols, fin):
        p, _ = place(k)
        wait(r.at[pl.ds(q, 2 * q), cols], recv.at[w, c, fin])
        add(t, base + p * q, [(r, q), (r, 2 * q)], q, cols)

    def ag_first(w, c, k, base, q, o, cols, rest):
        p, _ = place(k)
        h = q // 2
        s = ag_send.at[w]
        lo, hi = o.at[rows(base + p * q, h), cols], o.at[rows(base + p * q + h, h), cols]
        send(lo, lo, k, 1, s, recv.at[w, c, rest - 2])
        send(hi, hi, k, 3, s, recv.at[w, c, rest - 1])
        send(hi, hi, k, 1, s, recv.at[w, c, rest])
        send(lo, lo, k, 3, s, recv.at[w, c, rest])

    def ag_middle(w, c, k, base, q, o, cols, rest):
        p, _ = place(k)
        h = q // 2
        s = ag_send.at[w]
        lo = o.at[rows(base + (p + 3) % 4 * q, h), cols]
        hi = o.at[rows(base + (p + 1) % 4 * q + h, h), cols]
        wait(lo, recv.at[w, c, rest - 2])
        send(lo, lo, k, 1, s, recv.at[w, c, rest])
        wait(hi, recv.at[w, c, rest - 1])
        send(hi, hi, k, 3, s, recv.at[w, c, rest])

    def ag_last(w, c, q, o, cols, rest):
        wait(o.at[pl.ds(0, 2 * q), cols], recv.at[w, c, rest])

    def stage(j, w):
        t, o = T.at[w % SLOTS], O.at[w]
        r1, r2, r3 = R1.at[w], R2.at[w], R3.at[w]
        if j == 10:
            for c, ks, cols in colours(w):
                ag_last(w, c, 256, o, cols, REST1)
            o_copy(w).start()
            return
        for c, (k0, k1, k2), cols in colours(w):
            p0, p1, p2 = place(k0)[0], place(k1)[0], place(k2)[0]
            b1 = p0 * 256
            b2 = b1 + p1 * 64
            own = b2 + p2 * 16
            if j == 0:
                rs_first(w, c, k0, 0, 256, t, r1, cols, FIN)
            elif j == 1:
                rs_middle(w, c, k0, 0, 256, t, r1, cols, FIN)
            elif j == 2:
                rs_last(w, c, k0, 0, 256, t, r1, cols, FIN)
                rs_first(w, c, k1, b1, 64, t, r2, cols, FIN2)
            elif j == 3:
                rs_middle(w, c, k1, b1, 64, t, r2, cols, FIN2)
            elif j == 4:
                rs_last(w, c, k1, b1, 64, t, r2, cols, FIN2)
                for d in (1, 2, 3):
                    send(
                        t.at[rows(b2 + (p2 + d) % 4 * 16, 16), cols], r3.at[pl.ds((d - 1) * 16, 16), cols],
                        k2, d, rs_send.at[w], recv.at[w, c, RS3],
                    )
            elif j == 5:
                wait(r3.at[:, cols], recv.at[w, c, RS3])
                add(t, own, [(r3, 0), (r3, 16), (r3, 32)], 16, cols, o)
                mine = o.at[rows(own, 16), cols]
                for d in (1, 2, 3):
                    send(mine, mine, k2, d, ag_send.at[w], recv.at[w, c, AG3])
            elif j == 6:
                wait(r3.at[:, cols], recv.at[w, c, AG3])
                ag_first(w, c, k1, b1, 64, o, cols, REST2)
            elif j == 7:
                ag_middle(w, c, k1, b1, 64, o, cols, REST2)
            elif j == 8:
                ag_last(w, c, 64, o, cols, REST2)
                ag_first(w, c, k0, 0, 256, o, cols, REST1)
            elif j == 9:
                ag_middle(w, c, k0, 0, 256, o, cols, REST1)

    for i in range(2):
        a_copy(0, i).start()
    for j in range(GBUF - 1):
        g_copy(j).start()
    pl.semaphore_wait(barrier, 9)

    steps = waves * SUBS

    def tick(w, _):
        for s in range(SUBS):
            j = w * SUBS + s

            @pl.when(w < waves)
            def _():
                if s == 0:
                    @pl.when(w % per == 0)
                    def _():
                        turn(w // per)

                    @pl.when(w % per == 1)
                    def _():
                        @pl.when(w // per + 1 < waves // per)
                        def _():
                            for i in range(2):
                                a_copy(w // per + 1, i).start()

                    @pl.when(w >= SLOTS)
                    def _():
                        wait(T.at[w % SLOTS, pl.ds(0, 1008), :], rs_send.at[w - SLOTS])

                @pl.when(j + GBUF - 1 < steps)
                def _():
                    g_copy(j + GBUF - 1).start()

                g_copy(j).wait()
                T[w % SLOTS, :, s * NB:(s + 1) * NB] = jnp.dot(
                    at[...], gbuf[j % GBUF], preferred_element_type=F32
                ).astype(BF16)

            for i in reversed(range(11)):
                if (SUBS - 1 + i) % SUBS == s:
                    v = w - (SUBS - 1 + i) // SUBS

                    @pl.when((v >= 0) & (v < waves))
                    def _():
                        stage(i, v)
        return 0

    lax.fori_loop(0, waves + (SUBS - 1 + 10) // SUBS, tick, 0)

    def finish(w, _):
        @pl.when(w >= waves - SLOTS)
        def _():
            wait(T.at[w % SLOTS, pl.ds(0, 1008), :], rs_send.at[w])

        wait(O.at[w, pl.ds(0, 1008), :], ag_send.at[w])
        o_copy(w).wait()
        return 0

    lax.fori_loop(0, waves, finish, 0)


def solution(mesh):
    def body(a, g):
        _, mats, tokens, d = a.shape
        ff = g.shape[3]
        per = ff // WAVE
        waves = mats * per
        dma = pltpu.SemaphoreType.DMA
        return pl.pallas_call(
            functools.partial(kernel, waves, per),
            name="sums",
            out_shape=jax.ShapeDtypeStruct((mats, d, ff), BF16),
            in_specs=[pl.BlockSpec(memory_space=pl.ANY)] * 2,
            out_specs=pl.BlockSpec(memory_space=pl.ANY),
            scratch_shapes=[
                pltpu.VMEM((d, tokens), BF16),
                pltpu.VMEM((2, KB, d), BF16),
                pltpu.VMEM((GBUF, tokens, NB), BF16),
                pltpu.VMEM((SLOTS, d, WAVE), BF16),
                pltpu.VMEM((waves, 768, WAVE), BF16),
                pltpu.VMEM((waves, 192, WAVE), BF16),
                pltpu.VMEM((waves, 48, WAVE), BF16),
                pltpu.VMEM((waves, d, WAVE), BF16),
                dma((2,)),
                dma((GBUF,)),
                dma((waves,)),
                dma((waves,)),
                dma((waves,)),
                dma((waves, 3, 14)),
            ],
            compiler_params=pltpu.CompilerParams(
                collective_id=0, has_side_effects=True, vmem_limit_bytes=67_043_328
            ),
            cost_estimate=pl.CostEstimate(
                flops=2 * mats * tokens * d * ff, bytes_accessed=2 * mats * tokens * (d + ff), transcendentals=0
            ),
        )(a, g)

    return jax.shard_map(
        body, mesh=mesh, in_specs=P(("rep", "dp"), None, None, None), out_specs=P("rep", None, None), check_vma=False
    )
```

time: 819 us -> 216 us (0.26)
  blocking collectives: 740 us -> 0 us
  Pallas kernels: 0 us -> 202 us
  matrix products: 79.2 us -> 0 us
  local copies, waits for them, and re-layouts: 0 us -> 14.1 us
    dot_general x1 -> x0, blocking collectives: 740 us -> none  [step(): jnp.einsum('rsntd,rsntf->rndf', a, g, preferred_element_type=jnp.float32)]
    pallas_call x0 -> x1, Pallas kernels: none -> 202 us  [body(): pl.pallas_call(functools.partial(kernel, waves, per), name='sums', out_sh...]
    dot_general x1 -> x0, matrix products: 79.2 us -> none  [step(): jnp.einsum('rsntd,rsntf->rndf', a, g, preferred_element_type=jnp.float32)]
    unnamed x0 -> x1, local copies, waits for them, and re-layouts: none -> 14.1 us
where the time goes in v1:
time: 216 us
  Pallas kernels  202 us (94%)
  local copies, waits for them, and re-layouts  14.1 us (7%)
    pallas_call x1, Pallas kernels, body(): pl.pallas_call(functools.partial(kernel, waves, per), name='sums', out_sh...  202 us
    unnamed x1, local copies, waits for them, and re-layouts  14.1 us

profile of v1, /device:TPU:0, one launch (start us, length us, event | category | flops | bytes accessed | tf_op | source)
XLA Modules:
  0.0 215.9 jit_solution(14730705890717331806)
XLA Ops:
  0.0 201.9 %sums.1 = bf16[2,1024,4096]{2,1,0:T(8,128)(2,1)} custom-call(bf16[1,2,4096,1024]{3,2,1,0:T(8,128)(2,1)} %a_hbm.1, bf16[1,2,4096,4096]{3,2,1,0:T(8,128)(2,1)} %g_hbm.1), custom_call_target="tpu_custom_call" | custom-call | flops 68719476736 | bytes 83886080 | tf_op jit(solution)/shard_map/sums/pallas_call | solution.py:278
  201.9 14.1 %copy.4 = bf16[2,1024,4096]{2,1,0:T(8,128)(2,1)} copy(bf16[2,1024,4096]{2,1,0:T(8,128)(2,1)} %sums.1) | data formatting | bytes 33554432

commit v2 on v0

v2 whole, which is shorter than its diff:
```python
import functools

import jax
import jax.numpy as jnp
from jax import lax
from jax.experimental import pallas as pl
from jax.experimental.pallas import tpu as pltpu
from jax.sharding import PartitionSpec as P

F32, BF16 = jnp.float32, jnp.bfloat16

WAVE = 512
NB = 512
SUBS = WAVE // NB
WIDTHS = (128, 128, 256)
STARTS = (0, 128, 256)
SLOTS = 9
GBUF = 2
ABUF = 4
KB = 512
STAGES = tuple(
    (name, c, first, 1)
    for name, first in (
        ("rs1a", 0), ("ag3", 5), ("rs3", 4), ("rs2c", 3), ("rs2a", 2), ("ag2a", 6), ("ag2c", 7), ("rs1c", 1), ("rs1b", 0),
        ("ag1a", 8), ("ag1b", 8), ("ag1c", 9), ("done", 10),
    )
    for c in range(3)
)
A_L, A_R, FIN, B_L, B_R, FIN2, RS3, AG3, F2_L, F2_R, REST2, F1_L, F1_R, REST1 = range(14)


def kernel(
    waves, per, a_hbm, g_hbm, O,
    at, abuf, gbuf, T, R1, R2, R3,
    a_sem, g_sem, rs_send, ag_send, recv,
):
    rep, me = lax.axis_index("rep"), lax.axis_index("dp")
    tokens = a_hbm.shape[2]

    coords = (lax.div(me, 16), lax.rem(lax.div(me, 4), 4), lax.rem(me, 4))
    spot = tuple(tuple(lax.rem(p + d, 4) for p in coords) for d in range(4))
    peer = tuple(tuple(me + (spot[d][k] - coords[k]) * (16, 4, 1)[k] for k in range(3)) for d in range(4))

    barrier = pltpu.get_barrier_semaphore()
    for k in range(3):
        for d in (1, 2, 3):
            pl.semaphore_signal(barrier, inc=1, device_id={"dp": peer[d][k]})

    def a_copy(n, i):
        return pltpu.make_async_copy(
            a_hbm.at[0, n, pl.ds(pl.multiple_of(i * KB, KB), KB), :], abuf.at[lax.rem(i, ABUF)], a_sem.at[lax.rem(i, ABUF)]
        )

    def g_copy(j):
        w, s = lax.div(j, SUBS), lax.rem(j, SUBS)
        n = lax.div(w, per)
        col = pl.multiple_of((lax.rem(w, per)) * WAVE + s * NB, NB)
        return pltpu.make_async_copy(g_hbm.at[0, n, :, pl.ds(col, NB)], gbuf.at[lax.rem(j, GBUF)], g_sem.at[lax.rem(j, GBUF)])

    def place_out(w):
        return lax.div(w, per), (lax.rem(w, per)) * WAVE

    def turn(n):
        pieces = tokens // KB

        def piece(i, _):
            a_copy(n, i).wait()
            at[:, pl.ds(pl.multiple_of(i * KB, KB), KB)] = abuf[lax.rem(i, ABUF)].T

            @pl.when(i + ABUF < pieces)
            def _():
                a_copy(n, i + ABUF).start()

            return 0

        lax.fori_loop(0, pieces, piece, 0)

    def send(src, dst, to, ssem, rsem):
        pltpu.make_async_remote_copy(
            src_ref=src, dst_ref=dst, send_sem=ssem, recv_sem=rsem, device_id={"dp": to},
        ).start()

    def wait(ref, sem):
        pltpu.make_async_copy(ref, ref, sem).wait()

    def rows(start, size):
        return pl.ds(pl.multiple_of(start, 16), size)

    def add(dst, drow, srcs, n, cols, out=None, out_cols=None):
        out, out_cols = (dst, cols) if out is None else (out, out_cols)
        step = min(n, 128)

        def body(i, _):
            o = i * step
            total = dst[rows(drow + o, step), cols].astype(F32)
            for ref, row in srcs:
                total = total + ref[rows(row + o, step), cols].astype(F32)
            out[rows(drow + o, step), out_cols] = total.astype(BF16)
            return 0

        if n == step:
            body(0, 0)
        else:
            lax.fori_loop(0, n // step, body, 0)

    class Axis:
        def __init__(self, r, c, i):
            self.pick = lambda v: jnp.where(
                r == 0, v[(c + i) % 3], jnp.where(r == 1, v[(c + i + 1) % 3], v[(c + i + 2) % 3])
            )

        def at(self, d):
            return self.pick(spot[d])

        def to(self, d):
            return self.pick(peer[d])

    def rs_first(x, base, q, t, r, cols, s, al, ar):
        h = q // 2
        row = base + x.at(2) * q
        send(t.at[rows(row, h), cols], r.at[pl.ds(0, h), cols], x.to(1), s, al)
        send(t.at[rows(row + h, h), cols], r.at[pl.ds(h, h), cols], x.to(3), s, ar)

    def rs_second(x, base, q, t, r, cols, s, fin):
        h = q // 2
        send(t.at[rows(base + x.at(1) * q + h, h), cols], r.at[pl.ds(3 * h, h), cols], x.to(1), s, fin)
        send(t.at[rows(base + x.at(3) * q, h), cols], r.at[pl.ds(4 * h, h), cols], x.to(3), s, fin)

    def rs_middle(x, base, q, t, r, cols, s, al, ar, fin):
        h = q // 2
        one, two = base + x.at(1) * q, base + x.at(3) * q + h
        wait(r.at[pl.ds(0, h), cols], al)
        add(t, one, [(r, 0)], h, cols)
        wait(r.at[pl.ds(h, h), cols], ar)
        add(t, two, [(r, h)], h, cols)
        send(t.at[rows(one, h), cols], r.at[pl.ds(2 * h, h), cols], x.to(1), s, fin)
        send(t.at[rows(two, h), cols], r.at[pl.ds(5 * h, h), cols], x.to(3), s, fin)

    def rs_last(x, base, q, t, r, cols, fin):
        wait(r.at[pl.ds(q, 2 * q), cols], fin)
        add(t, base + x.at(0) * q, [(r, q), (r, 2 * q)], q, cols)

    def ag_parts(x, base, q, o, cols, d):
        h = q // 2
        row = base + x.at(d) * q
        return o.at[rows(row, h), cols], o.at[rows(row + h, h), cols]

    def ag_first(x, base, q, o, cols, s, fl, fr):
        lo, hi = ag_parts(x, base, q, o, cols, 0)
        send(lo, lo, x.to(1), s, fl)
        send(hi, hi, x.to(3), s, fr)

    def ag_second(x, base, q, o, cols, s, rest):
        lo, hi = ag_parts(x, base, q, o, cols, 0)
        send(hi, hi, x.to(1), s, rest)
        send(lo, lo, x.to(3), s, rest)

    def ag_middle(x, base, q, o, cols, s, fl, fr, rest):
        lo, _ = ag_parts(x, base, q, o, cols, 3)
        _, hi = ag_parts(x, base, q, o, cols, 1)
        wait(lo, fl)
        send(lo, lo, x.to(1), s, rest)
        wait(hi, fr)
        send(hi, hi, x.to(3), s, rest)

    def ag_last(q, o, cols, rest):
        wait(o.at[pl.ds(0, 2 * q), cols], rest)

    def stage(name, c, w):
        n, col = place_out(w)
        t, o = T.at[lax.rem(w, SLOTS)], O.at[n]
        r1, r2, r3 = R1.at[w], R2.at[w], R3.at[w]
        turn_of = lax.rem(w + rep, 3)
        rs, ag = rs_send.at[w], ag_send.at[w]
        rv = recv.at[w, c]
        cols = pl.ds(STARTS[c], WIDTHS[c])
        ocols = pl.ds(pl.multiple_of(col + STARTS[c], 128), WIDTHS[c])
        x0, x1, x2 = (Axis(turn_of, c, i) for i in range(3))
        if name == "rs1a":
            rs_first(x0, 0, 256, t, r1, cols, rs, rv.at[A_L], rv.at[A_R])
        elif name == "rs1b":
            rs_second(x0, 0, 256, t, r1, cols, rs, rv.at[FIN])
        elif name == "rs1c":
            rs_middle(x0, 0, 256, t, r1, cols, rs, rv.at[A_L], rv.at[A_R], rv.at[FIN])
        elif name == "ag1b":
            ag_second(x0, 0, 256, o, ocols, ag, rv.at[REST1])
        elif name == "ag1c":
            ag_middle(x0, 0, 256, o, ocols, ag, rv.at[F1_L], rv.at[F1_R], rv.at[REST1])
        elif name == "ag1a":
            ag_last(64, o, ocols, rv.at[REST2])
            ag_first(x0, 0, 256, o, ocols, ag, rv.at[F1_L], rv.at[F1_R])
        elif name == "done":
            ag_last(256, o, ocols, rv.at[REST1])
        else:
            b1 = x0.at(0) * 256
            if name == "rs2a":
                rs_last(x0, 0, 256, t, r1, cols, rv.at[FIN])
                rs_first(x1, b1, 64, t, r2, cols, rs, rv.at[B_L], rv.at[B_R])
                rs_second(x1, b1, 64, t, r2, cols, rs, rv.at[FIN2])
            elif name == "rs2c":
                rs_middle(x1, b1, 64, t, r2, cols, rs, rv.at[B_L], rv.at[B_R], rv.at[FIN2])
            elif name == "ag2a":
                wait(r3.at[:, cols], rv.at[AG3])
                ag_first(x1, b1, 64, o, ocols, ag, rv.at[F2_L], rv.at[F2_R])
                ag_second(x1, b1, 64, o, ocols, ag, rv.at[REST2])
            elif name == "ag2c":
                ag_middle(x1, b1, 64, o, ocols, ag, rv.at[F2_L], rv.at[F2_R], rv.at[REST2])
            elif name == "rs3":
                rs_last(x1, b1, 64, t, r2, cols, rv.at[FIN2])
                b2 = b1 + x1.at(0) * 64
                for d in (1, 2, 3):
                    piece = t.at[rows(b2 + x2.at(d) * 16, 16), cols]
                    send(piece, r3.at[pl.ds((d - 1) * 16, 16), cols], x2.to(d), rs, rv.at[RS3])
            elif name == "ag3":
                own = b1 + x1.at(0) * 64 + x2.at(0) * 16
                wait(r3.at[:, cols], rv.at[RS3])
                add(t, own, [(r3, 0), (r3, 16), (r3, 32)], 16, cols, o, ocols)
                mine = o.at[rows(own, 16), ocols]
                for d in (1, 2, 3):
                    send(mine, mine, x2.to(d), ag, rv.at[AG3])

    for i in range(ABUF):
        a_copy(0, i).start()
    for j in range(GBUF - 1):
        g_copy(j).start()
    pl.semaphore_wait(barrier, 9)

    steps = waves * SUBS

    def tick(j, _):
        @pl.when(j < steps)
        def _():
            w, s = lax.div(j, SUBS), lax.rem(j, SUBS)

            @pl.when(s == 0)
            def _():
                @pl.when(lax.rem(w, per) == 0)
                def _():
                    turn(lax.div(w, per))

                @pl.when((lax.rem(w, per) == 1) & (lax.div(w, per) + 1 < waves // per))
                def _():
                    for i in range(ABUF):
                        a_copy(lax.div(w, per) + 1, i).start()

                @pl.when(w >= SLOTS)
                def _():
                    wait(T.at[lax.rem(w, SLOTS), pl.ds(0, 1008), :], rs_send.at[w - SLOTS])

            @pl.when(j + GBUF - 1 < steps)
            def _():
                g_copy(j + GBUF - 1).start()

            g_copy(j).wait()
            T[lax.rem(w, SLOTS), :, pl.ds(pl.multiple_of(s * NB, NB), NB)] = jnp.dot(
                at[...], gbuf[lax.rem(j, GBUF)], preferred_element_type=F32
            ).astype(BF16)

        for name, c, first, every in STAGES:
            v, odd = lax.div(j - first, every), lax.rem(j - first, every)

            @pl.when((j >= first) & (odd == 0) & (v < waves))
            def _():
                stage(name, c, v)

        return 0

    lax.fori_loop(0, 1 + max(first + every * (waves - 1) for _, _, first, every in STAGES), tick, 0)

    def finish(w, _):
        @pl.when(w >= waves - SLOTS)
        def _():
            wait(T.at[lax.rem(w, SLOTS), pl.ds(0, 1008), :], rs_send.at[w])

        n, col = place_out(w)
        wait(O.at[n, pl.ds(0, 1008), pl.ds(pl.multiple_of(col, WAVE), WAVE)], ag_send.at[w])
        return 0

    lax.fori_loop(0, waves, finish, 0)


def solution(mesh):
    def body(a, g):
        _, mats, tokens, d = a.shape
        ff = g.shape[3]
        per = ff // WAVE
        waves = mats * per
        dma = pltpu.SemaphoreType.DMA
        return pl.pallas_call(
            functools.partial(kernel, waves, per),
            name="sums",
            out_shape=pltpu.VMEM((mats, d, ff), BF16),
            in_specs=[pl.BlockSpec(memory_space=pl.ANY)] * 2,
            out_specs=pl.BlockSpec(memory_space=pltpu.VMEM),
            scratch_shapes=[
                pltpu.VMEM((d, tokens), BF16),
                pltpu.VMEM((ABUF, KB, d), BF16),
                pltpu.VMEM((GBUF, tokens, NB), BF16),
                pltpu.VMEM((SLOTS, d, WAVE), BF16),
                pltpu.VMEM((waves, 768, WAVE), BF16),
                pltpu.VMEM((waves, 192, WAVE), BF16),
                pltpu.VMEM((waves, 48, WAVE), BF16),
                dma((ABUF,)),
                dma((GBUF,)),
                dma((waves,)),
                dma((waves,)),
                dma((waves, 3, 14)),
            ],
            compiler_params=pltpu.CompilerParams(
                collective_id=0, has_side_effects=True, vmem_limit_bytes=49_500_000
            ),
            cost_estimate=pl.CostEstimate(
                flops=2 * mats * tokens * d * ff, bytes_accessed=2 * mats * tokens * (d + ff), transcendentals=0
            ),
        )(a, g)

    return jax.shard_map(
        body, mesh=mesh, in_specs=P(("rep", "dp"), None, None, None), out_specs=P("rep", None, None), check_vma=False
    )
```

time: 819 us -> 170 us (0.21)
  blocking collectives: 740 us -> 0 us
  Pallas kernels: 0 us -> 163 us
  matrix products: 79.2 us -> 0 us
    dot_general x1 -> x0, blocking collectives: 740 us -> none  [step(): jnp.einsum('rsntd,rsntf->rndf', a, g, preferred_element_type=jnp.float32)]
    pallas_call x0 -> x1, Pallas kernels: none -> 163 us  [body(): pl.pallas_call(functools.partial(kernel, waves, per), name='sums', out_sh...]
    dot_general x1 -> x0, matrix products: 79.2 us -> none  [step(): jnp.einsum('rsntd,rsntf->rndf', a, g, preferred_element_type=jnp.float32)]
where the time goes in v2:
time: 170 us; the launch traced here: 169 us
  Pallas kernels  163 us (96%)
  local copies, waits for them, and re-layouts  6.16 us (4%)
    pallas_call x1, Pallas kernels, body(): pl.pallas_call(functools.partial(kernel, waves, per), name='sums', out_sh...  163 us
    unnamed x1, local copies, waits for them, and re-layouts  6.16 us

profile of v2, /device:TPU:0, one launch (start us, length us, event | category | flops | bytes accessed | tf_op | source)
XLA Modules:
  0.0 169.4 jit_solution(14080749553367681628)
XLA Ops:
  0.0 163.3 %sums.1 = bf16[2,1024,4096]{2,1,0:T(8,128)(2,1)S(1)} custom-call(bf16[1,2,4096,1024]{3,2,1,0:T(8,128)(2,1)} %a_hbm.1, bf16[1,2,4096,4096]{3,2,1,0:T(8,128)(2,1)} %g_hbm.1), custom_call_target="tpu_custom_call" | custom-call | flops 68719476736 | bytes 83886080 | tf_op jit(solution)/shard_map/sums/pallas_call | solution.py:289
  163.3 6.2 %copy.4 = bf16[2,1024,4096]{2,1,0:T(8,128)(2,1)} copy(bf16[2,1024,4096]{2,1,0:T(8,128)(2,1)S(1)} %sums.1) | data formatting | bytes 33554432

commit v3 on v2

--- a/solution.py
+++ b/solution.py
@@ -21,8 +21,8 @@
 STAGES = tuple(
     (name, c, first, 1)
     for name, first in (
-        ("rs1a", 0), ("ag3", 5), ("rs3", 4), ("rs2c", 3), ("rs2a", 2), ("ag2a", 6), ("ag2c", 7), ("rs1c", 1), ("rs1b", 0),
-        ("ag1a", 8), ("ag1b", 8), ("ag1c", 9), ("done", 10),
+        ("rs1a", 0), ("rs1c", 1), ("ag3", 5), ("rs3", 4), ("rs2c", 3), ("rs2a", 2), ("ag2a", 6), ("ag2c", 7), ("rs1b", 0),
+        ("ag1a", 8), ("ag1b", 8), ("ag1c", 10), ("done", 12),
     )
     for c in range(3)
 )

time: 170 us -> 168 us (0.988)
  no operation moved by 1% of the time
where the time goes in v3:
time: 168 us
  Pallas kernels  162 us (96%)
  local copies, waits for them, and re-layouts  6.16 us (4%)
    pallas_call x1, Pallas kernels, body(): pl.pallas_call(functools.partial(kernel, waves, per), name='sums', out_sh...  162 us
    unnamed x1, local copies, waits for them, and re-layouts  6.16 us

profile of v3, /device:TPU:0, one launch (start us, length us, event | category | flops | bytes accessed | tf_op | source)
XLA Modules:
  0.0 168.1 jit_solution(7863905493891016187)
XLA Ops:
  0.0 161.9 %sums.1 = bf16[2,1024,4096]{2,1,0:T(8,128)(2,1)S(1)} custom-call(bf16[1,2,4096,1024]{3,2,1,0:T(8,128)(2,1)} %a_hbm.1, bf16[1,2,4096,4096]{3,2,1,0:T(8,128)(2,1)} %g_hbm.1), custom_call_target="tpu_custom_call" | custom-call | flops 68719476736 | bytes 83886080 | tf_op jit(solution)/shard_map/sums/pallas_call | solution.py:289
  161.9 6.2 %copy.4 = bf16[2,1024,4096]{2,1,0:T(8,128)(2,1)} copy(bf16[2,1024,4096]{2,1,0:T(8,128)(2,1)S(1)} %sums.1) | data formatting | bytes 33554432
